TPU v7x, 32 devices: a whole 2x2x4 slice. The times are simulated.
32 devices in a mesh: groups: 1, seq: 1, row: 16 (over z, y, core), col: 2 (over x).
Axes of the slice: x: 2, y: 2, z: 4, core: 2. Of those that a mesh axis runs over, the one named last changes fastest.
Arguments:
- paired_left: bfloat16 [512, 32, 512], P(('groups', 'seq', 'col'), None, 'row'), may hold values from -24 to 24
- paired_right: bfloat16 [512, 32, 512], P(('groups', 'seq', 'row'), None, 'col'), may hold values from -24 to 24
- unpaired_left: bfloat16 [1024, 32, 512], P(('groups', 'seq', 'col'), None, 'row'), may hold values from -24 to 24
- unpaired_right: bfloat16 [1024, 32, 512], P(('groups', 'seq', 'row'), None, 'col'), may hold values from -24 to 24
- out_weight: bfloat16 [1024, 128], replicated, may hold values from -0.1875 to 0.1875
- out_bias: float32 [128], replicated, may hold values from -6 to 6
- chain_lengths: int32 [12], P('groups'), may hold values from 1 to 128, 512 in all
- unpaired_depths: int32 [12], P('groups'), may hold values from 256 to 1024
Outputs:
- pair_update: bfloat16 [512, 512, 128], P(('groups', 'row'), ('col', 'seq'))
Inputs may be any that keep to these rules, and one draw needn't show every extreme that they name: `chain_lengths`: chain lengths sum to 512. `unpaired_depths`: rows of the unpaired MSA at or beyond a chain's depth are padding.
All inputs are finite; a program needn't handle non-finite values.
Results may differ from a plain program's by a relative error of at most 0.0034.
Values may be sent and summed in bfloat16 or wider, within the bound.
A program may use at most 128 MiB of HBM per device.

v0:
```python
import functools

import jax
import jax.numpy as jnp
from jax import lax
from jax.experimental import pallas as pl
from jax.experimental.pallas import tpu as pltpu
from jax.sharding import PartitionSpec as P

LANES = 128
D_STEP = 8
WIDTH = D_STEP * LANES
LONGEST_CHAIN = 128
MESH = pl.DeviceIdType.MESH
Y_SIZE, CORES = 2, 2
AHEAD = 2
UP, DOWN, ACROSS, SIBLING = range(4)
PAIR, FREE = range(2)


def both(*terms):
    terms = [t for t in terms if t is not True]
    if any(t is False for t in terms):
        return False
    return functools.reduce(lambda a, b: a & b, terms) if terms else True


def guarded(condition, do):
    if condition is True:
        do()
    elif condition is not False:
        pl.when(condition)(do)


def fused_kernel(
    depth, width, group, paired_total, final,
    start_ref, end_ref, depth_ref,
    pair_in, free_in, left_pair_in, left_free_in, weight, bias,
    out_ref,
    pair_buf, free_buf, left_pair, left_free, outer_scr, free_scr, acc,
    send_sem, recv_sem, left_send, left_recv, local_sem,
):
    row, col = lax.axis_index("row"), lax.axis_index("col")
    core, y, z = row % CORES, (row // CORES) % Y_SIZE, row // (CORES * Y_SIZE)
    other = 1 - y
    rows, cols = out_ref.shape[0], out_ref.shape[1]
    channels = left_pair.shape[1] // rows
    tiles = cols // LANES
    steps = channels // D_STEP
    chunks = tiles * steps
    plane = rows * CORES * Y_SIZE
    span = group * channels

    def row_of(z_at, y_at, core_at):
        return (z_at * Y_SIZE + y_at) * CORES + core_at

    up, down = row_of(z + 1, y, core), row_of(z - 1, y, core)
    across, sibling = row_of(z, other, core), row_of(z, y, 1 - core)
    has_up, has_down = z < depth - 1, z > 0

    barrier = pltpu.get_barrier_semaphore()

    def greet(axis, at):
        pl.semaphore_signal(barrier, inc=1, device_id={axis: at}, device_id_type=MESH)

    pl.when(has_up)(lambda: greet("row", up))
    pl.when(has_down)(lambda: greet("row", down))
    greet("row", across)
    greet("row", sibling)
    for shift in range(1, width):
        greet("col", lax.rem(col + shift, width))
    pl.semaphore_wait(barrier, jnp.where(has_up, 1, 0) + jnp.where(has_down, 1, 0) + 2 + width - 1)

    def tile_of(chunk):
        turn = chunk // steps
        return jnp.where(col * 2 >= width, tiles - 1 - turn, turn)

    def offset(chunk):
        return pl.multiple_of((tile_of(chunk) * steps + chunk % steps) * WIDTH, WIDTH)

    def reach(kind, chunk):
        if kind == PAIR:
            return 0, depth - 1
        first = (col * tiles + tile_of(chunk)) * LANES
        lowest = jnp.maximum(first - (LONGEST_CHAIN - 1), 0) // plane
        highest = jnp.minimum(first + LANES - 1 + (LONGEST_CHAIN - 1), depth * plane - 1) // plane
        return lowest, highest

    def needed(kind, chunk):
        if kind == PAIR:
            return True
        lowest, highest = reach(kind, chunk)
        return (z >= lowest) & (z <= highest)

    def early(kind, chunk):
        return chunk % 2 == 1 if kind == PAIR else False

    sources, buffers = (pair_in, free_in), (pair_buf, free_buf)

    def copy(kind, chunk, way, origin, target, own):
        part = pl.ds(offset(chunk), WIDTH)
        here = buffers[kind].at[origin, :, part]
        return pltpu.make_async_remote_copy(
            src_ref=sources[kind].at[:, part] if own else here, dst_ref=here,
            send_sem=send_sem.at[way, kind, chunk, origin // CORES], recv_sem=recv_sem.at[kind, chunk, origin],
            device_id={"row": target}, device_id_type=MESH)

    def forward(kind, chunk, z_at, y_at, started):
        origin = row_of(z_at, y_at, core)
        line = y_at is y
        own = line and z_at is z
        lowest, highest = reach(kind, chunk)
        soon = early(kind, chunk)
        wanted = needed(kind, chunk)

        def go(way, target):
            c = copy(kind, chunk, way, origin, target, own)
            c.start() if started else c.wait_send()

        along = True if line else soon
        guarded(both(has_up, z_at <= z, z < highest, along), lambda: go(UP, up))
        guarded(both(has_down, z_at >= z, z > lowest, along), lambda: go(DOWN, down))
        if own:
            guarded(wanted, lambda: go(ACROSS, across))
        elif line:
            guarded(both(wanted, True if soon is False else jnp.logical_not(soon)), lambda: go(ACROSS, across))
        guarded(wanted, lambda: go(SIBLING, sibling))

    def arrive(kind, chunk, z_at, y_at, core_at):
        origin = row_of(z_at, y_at, core_at)
        copy(kind, chunk, SIBLING, origin, sibling, False).wait_recv()

    def hops(hop):
        if hop == 0:
            return ((z, True, True),)
        return ((z - hop, z >= hop, True), (z + hop, z + hop < depth, False))

    def arrivals(chunk, visit):
        for hop in range(depth):
            for y_at in (y, other):
                if hop == 0 and y_at is y:
                    continue
                for kind in (PAIR, FREE):
                    lowest, highest = reach(kind, chunk)
                    for z_at, there, below in hops(hop):
                        if y_at is y and kind == FREE:
                            passes = (z <= highest) if below else (z >= lowest)
                        else:
                            passes = needed(kind, chunk)
                        guarded(both(there, passes), functools.partial(visit, kind, z_at, y_at))

    def issue(chunk):
        for kind in (PAIR, FREE):
            forward(kind, chunk, z, y, True)

    def relay(chunk):
        def visit(kind, z_at, y_at):
            arrive(kind, chunk, z_at, y_at, core)
            forward(kind, chunk, z_at, y_at, True)
        arrivals(chunk, visit)

    def drain(chunk):
        for kind in (PAIR, FREE):
            forward(kind, chunk, z, y, False)
        arrivals(chunk, lambda kind, z_at, y_at: forward(kind, chunk, z_at, y_at, False))

    def gathered(chunk):
        for kind in (PAIR, FREE):
            def every(kind=kind):
                for z_at in range(depth):
                    for y_at in range(Y_SIZE):
                        arrive(kind, chunk, z_at, y_at, 1 - core)
            guarded(needed(kind, chunk), every)

    for chunk in range(min(AHEAD, chunks)):
        issue(jnp.int32(chunk))

    left_copies = []
    local = [
        pltpu.make_async_copy(pair_in, pair_buf.at[row], local_sem.at[0]),
        pltpu.make_async_copy(free_in, free_buf.at[row], local_sem.at[1]),
    ]
    for n, (source, out) in enumerate(((left_pair_in, left_pair), (left_free_in, left_free))):
        mine = out.at[col]
        for shift in range(1, width):
            c = pltpu.make_async_remote_copy(
                src_ref=source, dst_ref=mine, send_sem=left_send.at[n, shift], recv_sem=left_recv.at[n, shift],
                device_id={"col": lax.rem(col + shift, width)}, device_id_type=MESH)
            c.start()
            left_copies.append(c)
        local.append(pltpu.make_async_copy(source, mine, local_sem.at[2 + n]))
    for c in local:
        c.start()

    def left(ref, at):
        return jnp.concatenate([ref[n, at, :] for n in range(width)], axis=1)

    def compute(chunk):
        gathered(chunk)
        step = chunk % steps
        tile = tile_of(chunk)
        part = pl.ds(offset(chunk), WIDTH)
        lanes = lax.broadcasted_iota(jnp.int32, (1, LANES), 1) + tile * LANES
        mask_on = needed(FREE, chunk)

        @pl.when(step == 0)
        def _():
            acc[...] = jnp.zeros_like(acc)

        w = weight[step]

        @pl.loop(0, rows // group)
        def _(g):
            base = g * group
            at = pl.ds(pl.multiple_of(base * channels, span), span)
            right = pair_buf[:, :, part].reshape(-1, WIDTH)
            outer_scr[...] = jnp.dot(left(left_pair, at), right, preferred_element_type=jnp.float32)

            @pl.when(mask_on)
            def _():
                right = free_buf[:, :, part].reshape(-1, WIDTH)
                free_scr[...] = jnp.dot(left(left_free, at), right, preferred_element_type=jnp.float32)
                for i in range(group):
                    same = (lanes >= start_ref[base + i]) & (lanes < end_ref[base + i])
                    piece = pl.ds(i * channels, channels)
                    for d in range(D_STEP):
                        at_lanes = pl.ds(d * LANES, LANES)
                        outer_scr[piece, at_lanes] += jnp.where(same, free_scr[piece, at_lanes], 0.0)

            for pair in range(group // 2):
                halves = []
                for i in (2 * pair, 2 * pair + 1):
                    mine = outer_scr[pl.ds(i * channels, channels), :].astype(jnp.bfloat16)
                    halves.append(jnp.concatenate(
                        [mine[:, d * LANES:(d + 1) * LANES] for d in range(D_STEP)], axis=0))
                projected = jnp.dot(
                    w, jnp.concatenate(halves, axis=1), preferred_element_type=jnp.float32)
                for k in range(2):
                    acc[base + 2 * pair + k] += projected[:, k * LANES:(k + 1) * LANES]

        @pl.when(step == steps - 1)
        def _():
            @pl.loop(0, rows)
            def _(i):
                same = (lanes >= start_ref[i]) & (lanes < end_ref[i])
                count = paired_total + jnp.where(same, depth_ref[i].astype(jnp.float32), 0.0)
                value = (acc[i] * (1.0 / count)).T
                if final:
                    value = value + bias[...]
                out_ref[i, pl.ds(pl.multiple_of(tile * LANES, LANES), LANES), :] = value.astype(out_ref.dtype)

    def done_after(turn):
        return jnp.where(turn < 3, 0, jnp.minimum(turn, 2 * (turn - 2)))

    @pl.loop(0, chunks + 1)
    def _(turn):
        pl.when(turn + AHEAD < chunks)(lambda: issue(turn + AHEAD))
        pl.when(turn < chunks)(lambda: relay(turn))

        @pl.when(turn == 3)
        def _():
            for c in left_copies:
                c.wait()
            for c in local:
                c.wait()

        @pl.loop(done_after(turn - 1), done_after(turn))
        def _(chunk):
            compute(chunk)

    @pl.loop(0, chunks)
    def _(chunk):
        drain(chunk)


def fused(right_pair, right_free, left_pair, left_free, weight, bias, start, end, depth, paired_total, final):
    count, width = lax.axis_size("row"), lax.axis_size("col")
    layers = count // (Y_SIZE * CORES)
    rows = start.shape[0]
    channels = left_pair.shape[0] // rows
    out_channels = weight.shape[1]
    cols = right_pair.shape[1] // channels
    chunks = cols // LANES * (channels // D_STEP)
    group = min(16, rows)
    smem = pl.BlockSpec(memory_space=pltpu.SMEM)
    vmem = pl.BlockSpec(memory_space=pltpu.VMEM)
    anywhere = pl.BlockSpec(memory_space=pl.ANY)
    return pl.pallas_call(
        functools.partial(fused_kernel, layers, width, group, float(paired_total), final),
        out_shape=jax.ShapeDtypeStruct((rows, cols, out_channels), jnp.bfloat16 if final else jnp.float32),
        in_specs=[smem] * 3 + [anywhere] * 4 + [vmem] * 2,
        out_specs=vmem,
        scratch_shapes=[
            pltpu.VMEM((count,) + right_pair.shape, jnp.bfloat16),
            pltpu.VMEM((count,) + right_free.shape, jnp.bfloat16),
            pltpu.VMEM((width,) + left_pair.shape, jnp.bfloat16),
            pltpu.VMEM((width,) + left_free.shape, jnp.bfloat16),
            pltpu.VMEM((group * channels, WIDTH), jnp.float32),
            pltpu.VMEM((group * channels, WIDTH), jnp.float32),
            pltpu.VMEM((rows, out_channels, LANES), jnp.float32),
            pltpu.SemaphoreType.DMA((4, 2, chunks, count // CORES)),
            pltpu.SemaphoreType.DMA((2, chunks, count)),
            pltpu.SemaphoreType.DMA((2, width)),
            pltpu.SemaphoreType.DMA((2, width)),
            pltpu.SemaphoreType.DMA((4,)),
        ],
        compiler_params=pltpu.CompilerParams(collective_id=0, has_side_effects=True, vmem_limit_bytes=60 << 20),
        name="gather_multiply",
    )(start, end, depth, right_pair, right_free, left_pair, left_free, weight, bias)


def flat_right(x):
    depth, channels, cols = x.shape
    return x.reshape(depth, channels, cols // LANES, LANES).transpose(0, 2, 1, 3).reshape(depth, -1)


def flat_left(x):
    depth, channels, rows = x.shape
    return x.transpose(2, 1, 0).reshape(rows * channels, depth)


def body(
    paired_left, paired_right, unpaired_left, unpaired_right,
    out_weight, out_bias, chain_lengths, unpaired_depths,
):
    channels, rows = paired_left.shape[1:]
    cols = paired_right.shape[2]
    first_row = lax.axis_index("row") * rows
    first_col = lax.axis_index("col") * cols
    positions = first_row + jnp.arange(rows, dtype=jnp.int32)
    chains = jnp.arange(chain_lengths.shape[0])
    chain_ends = jnp.sum(
        jnp.where(chains[None, :] <= chains[:, None], chain_lengths[None, :], 0), axis=1, dtype=jnp.int32)
    chain_starts = chain_ends - chain_lengths
    inside = (positions[:, None] >= chain_starts[None, :]) & (positions[:, None] < chain_ends[None, :])

    def pick(table):
        return jnp.sum(jnp.where(inside, table[None, :], 0), axis=1, dtype=jnp.int32)

    depth = pick(unpaired_depths)
    start = pick(chain_starts) - first_col
    end = pick(chain_ends) - first_col

    seq = lax.axis_size("seq")
    free_here = unpaired_left.shape[0]
    first_free = (lax.axis_index("seq") * lax.axis_size("col") + lax.axis_index("col")) * free_here
    free_ids = first_free + jnp.arange(free_here, dtype=jnp.int32)
    live = free_ids[:, None] < depth[None, :]
    masked = jnp.where(live[:, None, :], unpaired_left, jnp.zeros((), unpaired_left.dtype))

    out_channels = out_weight.shape[1]
    weight = out_weight.reshape(channels, channels // D_STEP, D_STEP, out_channels).transpose(1, 3, 2, 0)
    weight = weight.reshape(channels // D_STEP, out_channels, D_STEP * channels)
    bias = out_bias.reshape(1, -1)
    paired_total = paired_right.shape[0] * lax.axis_size("row") * seq
    out = fused(
        flat_right(paired_right), flat_right(unpaired_right), flat_left(paired_left), flat_left(masked),
        weight, bias, start, end, depth, paired_total, seq == 1)
    if seq == 1:
        return out
    summed = lax.psum(out, "seq")
    share = cols // seq
    own = lax.dynamic_slice_in_dim(summed, lax.axis_index("seq") * share, share, 1)
    return (own + bias).astype(jnp.bfloat16)


def solution(mesh):
    return jax.shard_map(
        body,
        mesh=mesh,
        in_specs=(
            P(("groups", "seq", "col"), None, "row"),
            P(("groups", "seq", "row"), None, "col"),
            P(("groups", "seq", "col"), None, "row"),
            P(("groups", "seq", "row"), None, "col"),
            P(),
            P(),
            P("groups"),
            P("groups"),
        ),
        out_specs=P(("groups", "row"), ("col", "seq"), None),
        check_vma=False,
    )
```

profile of v0, /device:TPU:0, one launch (start us, length us, event | category | flops | bytes accessed | tf_op | source)
XLA Modules:
  0.0 226.5 jit_solution(10284900597145258544)
XLA Ops:
  0.0 0.0 copy-start
  0.0 0.0 copy-start.2
  0.0 0.9 select_reduce_fusion.3
  0.9 0.7 sub.13
  1.6 0.7 select_reduce_fusion
  2.3 0.0 copy-start.3
  2.3 0.6 broadcast_subtract_fusion
  2.9 0.1 broadcast_compare_fusion
  3.0 0.0 copy-start.1
  3.0 1.1 copy.29
  4.2 0.8 copy.30.weight
  5.0 2.1 copy.27
  7.1 0.0 copy-done.2
  7.1 0.1 copy_bitcast_fusion.3
  7.2 1.1 copy.40
  8.4 0.0 copy-done.3
  8.4 0.0 copy-done.1
  8.4 0.1 select_bitcast_fusion
  8.5 1.6 copy.28
  10.0 0.0 copy-done
  10.0 0.2 copy_bitcast_fusion.1
  10.2 1.7 copy.39
  11.9 211.5 %gather_multiply.1 = bf16[32,256,128]{2,1,0:T(8,128)(2,1)} custom-call(s32[32]{0:T(128)} %get-tuple-element.9.start_ref, s32[32]{0:T(128)} %get-tuple-element.8.end_ref, s32[32]{0:T(128)} %copy-done.3, bf16[32,8192]{1,0:T(8,128)(2,1)} %bitcast.36, bf16[64,8192]{1,0:T(8,128)(2,1)} %bitcast.33, bf16[1024,256]{1,0:T(8,128)(2,1)} %bitcast.35, ...), custom_call_target="tpu_custom_call" | custom-call | tf_op jit(solution)/shard_map/gather_multiply/pallas_call | solution.py:288
  223.4 3.1 %copy.42 = bf16[32,256,128]{2,1,0:T(8,128)(2,1)} copy(bf16[32,256,128]{2,1,0:T(8,128)(2,1)} %gather_multiply.1) | data formatting | bytes 4194304
  (2 shorter events, 0.0 us)
Async XLA Ops:
  0.0 10.0 %copy-start = (bf16[64,32,256]{2,1,0:T(8,128)(2,1)S(1)}, bf16[64,32,256]{2,1,0:T(8,128)(2,1)}, u32[]{:S(2)}) copy-start(bf16[64,32,256]{2,1,0:T(8,128)(2,1)} %param.11) | copy-start | bytes 3145732
  0.0 7.1 %copy-start.2 = (bf16[32,32,256]{2,1,0:T(8,128)(2,1)S(1)}, bf16[32,32,256]{2,1,0:T(8,128)(2,1)}, u32[]{:S(2)}) copy-start(bf16[32,32,256]{2,1,0:T(8,128)(2,1)} %param.9) | copy-start | bytes 1572868
  2.3 6.1 %copy-start.3 = (s32[32]{0:T(128)}, s32[32]{0:T(128)S(1)}, u32[]{:S(2)}) copy-start(s32[32]{0:T(128)S(1)} %get-tuple-element.5.depth_ref) | copy-start | bytes 388
  3.0 5.4 %copy-start.1 = (bf16[512,32,32]{0,2,1:T(8,128)(2,1)S(1)}, bf16[512,32,32]{0,2,1:T(8,128)(2,1)}, u32[]{:S(2)}) copy-start(bf16[512,32,32]{0,2,1:T(8,128)(2,1)} %param.10) | copy-start | bytes 3145732
where the time goes:
time: 227 us
  Pallas kernels  211 us (93%)
  local copies, waits for them, and re-layouts  11.9 us (5%)
  other arithmetic  3.05 us (1%)
    pallas_call x1, Pallas kernels, fused(): pl.pallas_call(functools.partial(fused_kernel, layers, width, group, floa...  211 us
    unnamed x11, local copies, waits for them, and re-layouts  5.98 us

commit v1 on v0

v1 whole, which is shorter than its diff:
```python
import functools

import jax
import jax.numpy as jnp
from jax import lax
from jax.experimental import pallas as pl
from jax.experimental.pallas import tpu as pltpu
from jax.sharding import PartitionSpec as P

LANES = 128
D_STEP = 8
WIDTH = D_STEP * LANES
LONGEST_CHAIN = 128
MESH = pl.DeviceIdType.MESH
Y_SIZE, CORES = 2, 2
AHEAD = 2
PAIR_EARLY = 4
UP, DOWN, ACROSS, SIBLING = range(4)
PAIR, FREE = range(2)


def both(*terms):
    terms = [t for t in terms if t is not True]
    if any(t is False for t in terms):
        return False
    return functools.reduce(lambda a, b: a & b, terms) if terms else True


def guarded(condition, do):
    if condition is True:
        do()
    elif condition is not False:
        pl.when(condition)(do)


def fused_kernel(
    depth, width, group, paired_total, final, share,
    start_ref, end_ref, depth_ref,
    pair_in, free_in, left_pair_in, left_free_in, weight, bias,
    out_ref,
    pair_buf, free_buf, left_pair, left_free, outer_scr, free_scr, acc, help_acc, help_out, via_buf,
    send_sem, recv_sem, left_send, left_recv, local_sem, via_send, via_recv, pass_send, help_sem,
):
    row, col = lax.axis_index("row"), lax.axis_index("col")
    core, y, z = row % CORES, (row // CORES) % Y_SIZE, row // (CORES * Y_SIZE)
    other = 1 - y
    rows, cols = out_ref.shape[0], out_ref.shape[1]
    channels = left_pair.shape[1] // rows
    tiles = cols // LANES
    steps = channels // D_STEP
    chunks = tiles * steps
    plane = rows * CORES * Y_SIZE
    span = group * channels

    def row_of(z_at, y_at, core_at):
        return (z_at * Y_SIZE + y_at) * CORES + core_at

    up, down = row_of(z + 1, y, core), row_of(z - 1, y, core)
    across, sibling = row_of(z, other, core), row_of(z, y, 1 - core)
    has_up, has_down = z < depth - 1, z > 0
    first_plane = jnp.where(col == 0, 0, depth - 1)
    last_plane = depth - 1 - first_plane
    asks = z == first_plane if share else False
    helps = z == last_plane if share else False
    distant = jnp.abs(z - last_plane) > 1 if share else False

    barrier = pltpu.get_barrier_semaphore()

    def greet(axis, at):
        pl.semaphore_signal(barrier, inc=1, device_id={axis: at}, device_id_type=MESH)

    pl.when(has_up)(lambda: greet("row", up))
    pl.when(has_down)(lambda: greet("row", down))
    greet("row", across)
    greet("row", sibling)
    for shift in range(1, width):
        greet("col", lax.rem(col + shift, width))
    met = jnp.where(has_up, 1, 0) + jnp.where(has_down, 1, 0) + 2 + width - 1
    if share:
        for hop in range(2, depth):
            far = jnp.where(last_plane == 0, hop, depth - 1 - hop)
            pl.when(helps)(functools.partial(greet, "row", row_of(far, y, core)))
        met = met + jnp.where(distant, 1, 0)
    pl.semaphore_wait(barrier, met)

    def tile_of(chunk, at_col=col):
        turn = chunk % tiles
        return jnp.where(at_col * 2 >= width, turn, tiles - 1 - turn)

    def offset(chunk, at_col=col):
        return pl.multiple_of((tile_of(chunk, at_col) * steps + chunk // tiles) * WIDTH, WIDTH)

    def reach(kind, chunk):
        if kind == PAIR:
            return 0, depth - 1
        first = (col * tiles + tile_of(chunk)) * LANES
        lowest = jnp.maximum(first - (LONGEST_CHAIN - 1), 0) // plane
        highest = jnp.minimum(first + LANES - 1 + (LONGEST_CHAIN - 1), depth * plane - 1) // plane
        if share:
            shared = chunk % tiles == 0
            lowest = jnp.where(shared & (col == 0), jnp.maximum(lowest, 1), lowest)
            highest = jnp.where(shared & (col > 0), jnp.minimum(highest, depth - 2), highest)
        return lowest, highest

    def needed(kind, chunk):
        if kind == PAIR:
            return True
        lowest, highest = reach(kind, chunk)
        return (z >= lowest) & (z <= highest)

    def early(kind, chunk):
        if kind == PAIR:
            return chunk % PAIR_EARLY == 0
        return chunk % tiles == 0 if share else False

    def late(kind, chunk):
        soon = early(kind, chunk)
        return True if soon is False else jnp.logical_not(soon)

    sources, buffers = (pair_in, free_in), (pair_buf, free_buf)

    def copy(kind, chunk, way, origin, target, own):
        part = pl.ds(offset(chunk), WIDTH)
        here = buffers[kind].at[origin, :, part]
        return pltpu.make_async_remote_copy(
            src_ref=sources[kind].at[:, part] if own else here, dst_ref=here,
            send_sem=send_sem.at[way, kind, chunk, origin // CORES], recv_sem=recv_sem.at[kind, chunk, origin],
            device_id={"row": target}, device_id_type=MESH)

    def move(c, started):
        c.start() if started else c.wait_send()

    def forward(kind, chunk, z_at, y_at, started):
        origin = row_of(z_at, y_at, core)
        line = y_at is y
        own = line and z_at is z
        lowest, highest = reach(kind, chunk)
        soon = early(kind, chunk)
        wanted = needed(kind, chunk)

        def go(way, target):
            move(copy(kind, chunk, way, origin, target, own), started)

        along = True if line else soon
        guarded(both(has_up, z_at <= z, z < highest, along), lambda: go(UP, up))
        guarded(both(has_down, z_at >= z, z > lowest, along), lambda: go(DOWN, down))
        if own:
            guarded(wanted if wanted is True or soon is False else wanted | soon, lambda: go(ACROSS, across))
        elif line:
            guarded(both(wanted, late(kind, chunk)), lambda: go(ACROSS, across))
        guarded(wanted, lambda: go(SIBLING, sibling))

    def arrive(kind, chunk, z_at, y_at, core_at):
        origin = row_of(z_at, y_at, core_at)
        copy(kind, chunk, SIBLING, origin, sibling, False).wait_recv()

    def hops(hop):
        if hop == 0:
            return ((z, True, None),)
        return ((z - hop, z >= hop, True), (z + hop, z + hop < depth, False))

    def arrivals(hop, y_at, chunk, visit):
        for kind in (PAIR, FREE):
            lowest, highest = reach(kind, chunk)
            for z_at, there, below in hops(hop):
                passes = True
                if kind == FREE and below is not None:
                    passes = (z <= highest) if below else (z >= lowest)
                if y_at is not y and kind == FREE:
                    soon = early(kind, chunk)
                    if soon is False:
                        passes = needed(kind, chunk)
                    else:
                        passes = (soon & passes) | (jnp.logical_not(soon) & needed(kind, chunk))
                guarded(both(there, passes), functools.partial(visit, kind, z_at, y_at))

    def onward(chunk, started):
        def visit(kind, z_at, y_at):
            if started:
                arrive(kind, chunk, z_at, y_at, core)
            forward(kind, chunk, z_at, y_at, started)
        return visit

    def slot(part):
        return part * tiles + 1

    def helping(turn, do):
        part = turn - turn // 3
        pl.when((turn >= 0) & (turn % 3 < 2) & (part < steps))(lambda: do(part))

    def via_copy(part, straight):
        target = free_buf.at[row, :, pl.ds(offset(slot(part), 1 - col), WIDTH)] if straight else via_buf.at[part]
        return pltpu.make_async_remote_copy(
            src_ref=free_in.at[:, pl.ds(offset(part * tiles), WIDTH)], dst_ref=target,
            send_sem=via_send.at[part], recv_sem=via_recv.at[part], device_id={"col": 1 - col}, device_id_type=MESH)

    def pass_copy(part):
        return pltpu.make_async_remote_copy(
            src_ref=via_buf.at[part], dst_ref=free_buf.at[row, :, pl.ds(offset(slot(part)), WIDTH)],
            send_sem=pass_send.at[part], recv_sem=recv_sem.at[FREE, slot(part), row],
            device_id={"row": row_of(last_plane, y, core)}, device_id_type=MESH)

    def via(part, started):
        pl.when(asks)(lambda: move(via_copy(part, True), started))
        pl.when(jnp.logical_not(asks))(lambda: move(via_copy(part, False), started))

    def help_spread(part, z_at, y_at, started):
        origin = row_of(z_at, y_at, core)
        if y_at is y:
            move(copy(FREE, slot(part), ACROSS, origin, across, False), started)
        move(copy(FREE, slot(part), SIBLING, origin, sibling, False), started)

    def help_first(part, started):
        if started:
            via_copy(part, False).wait_recv()

        @pl.when(jnp.logical_not(helps))
        def _():
            move(pass_copy(part), started)

        @pl.when(helps)
        def _():
            help_spread(part, z, y, started)

    def help_line(part, started):
        @pl.when(helps)
        def _():
            for hop in range(1, depth):
                z_at = jnp.where(last_plane == 0, hop, depth - 1 - hop)
                if started:
                    arrive(FREE, slot(part), z_at, y, core)
                help_spread(part, z_at, y, started)

    def help_last(part, started):
        @pl.when(helps)
        def _():
            for hop in range(depth):
                z_at = jnp.where(last_plane == 0, hop, depth - 1 - hop)
                if started:
                    arrive(FREE, slot(part), z_at, other, core)
                help_spread(part, z_at, other, started)

    def result_copy():
        return pltpu.make_async_remote_copy(
            src_ref=help_out, dst_ref=help_out, send_sem=help_sem.at[0], recv_sem=help_sem.at[1],
            device_id={"col": 1 - col}, device_id_type=MESH)

    def issue(chunk, started=True):
        for kind in (PAIR, FREE):
            forward(kind, chunk, z, y, started)

    def within(chunk, limit, do):
        pl.when((chunk >= 0) & (chunk < limit))(lambda: do(chunk))

    def relay(turn):
        for hop in range(depth - 1, 0, -1):
            within(turn - (hop - 1), chunks, lambda chunk: arrivals(hop, y, chunk, onward(chunk, True)))
        if share:
            helping(turn, lambda part: help_first(part, True))
            helping(turn - 1, lambda part: help_line(part, True))
        for hop in range(depth - 1, -1, -1):
            within(turn - hop, chunks, lambda chunk: arrivals(hop, other, chunk, onward(chunk, True)))
        if share:
            helping(turn - 2, lambda part: help_last(part, True))
            helping(turn + AHEAD, lambda part: via(part, True))
        within(turn + AHEAD, chunks, issue)

    def drain(chunk):
        issue(chunk, False)
        for hop in range(depth):
            if hop:
                arrivals(hop, y, chunk, onward(chunk, False))
            arrivals(hop, other, chunk, onward(chunk, False))
        if share:
            @pl.when(chunk < steps)
            def _():
                via(chunk, False)
                help_first(chunk, False)
                help_line(chunk, False)
                help_last(chunk, False)

    def from_sibling(kind, chunk):
        for z_at in range(depth):
            for y_at in range(Y_SIZE):
                arrive(kind, chunk, z_at, y_at, 1 - core)

    def gathered(chunk):
        for kind in (PAIR, FREE):
            guarded(needed(kind, chunk), functools.partial(from_sibling, kind, chunk))

    for chunk in range(min(AHEAD, chunks)):
        if share:
            helping(jnp.int32(chunk), lambda part: via(part, True))
        issue(jnp.int32(chunk))

    left_copies = []
    local = [pltpu.make_async_copy(pair_in, pair_buf.at[row], local_sem.at[0])]
    own_free = pltpu.make_async_copy(free_in, free_buf.at[row], local_sem.at[1])
    unhelping = jnp.logical_not(helps) if share else True
    for n, (source, out) in enumerate(((left_pair_in, left_pair), (left_free_in, left_free))):
        mine = out.at[col]
        for shift in range(1, width):
            c = pltpu.make_async_remote_copy(
                src_ref=source, dst_ref=mine, send_sem=left_send.at[n, shift], recv_sem=left_recv.at[n, shift],
                device_id={"col": lax.rem(col + shift, width)}, device_id_type=MESH)
            c.start()
            left_copies.append(c)
        local.append(pltpu.make_async_copy(source, mine, local_sem.at[2 + n]))
    for c in local:
        c.start()
    guarded(unhelping, own_free.start)

    def left(ref, at):
        return jnp.concatenate([ref[n, at, :] for n in range(width)], axis=1)

    def same_at(first, i):
        lanes = lax.broadcasted_iota(jnp.int32, (1, LANES), 1) + first * LANES
        return (lanes >= start_ref[i]) & (lanes < end_ref[i])

    def project(w, scratch, total, base):
        for pair in range(group // 2):
            halves = []
            for i in (2 * pair, 2 * pair + 1):
                mine = scratch[pl.ds(i * channels, channels), :].astype(jnp.bfloat16)
                halves.append(jnp.concatenate(
                    [mine[:, d * LANES:(d + 1) * LANES] for d in range(D_STEP)], axis=0))
            projected = jnp.dot(w, jnp.concatenate(halves, axis=1), preferred_element_type=jnp.float32)
            for k in range(2):
                total[base + 2 * pair + k] += projected[:, k * LANES:(k + 1) * LANES]

    def compute(chunk):
        if tiles > 1:
            @pl.when(chunk == chunks - 1)
            def _():
                for done in range(tiles - 1):
                    finish(done)

        gathered(chunk)
        step = chunk // tiles
        turn = chunk % tiles
        first = col * tiles + tile_of(chunk)
        part = pl.ds(offset(chunk), WIDTH)
        mask_on = needed(FREE, chunk)
        total = acc.at[turn]
        w = weight[step]

        @pl.when(step == 0)
        def _():
            total[...] = jnp.zeros_like(total)

        @pl.loop(0, rows // group)
        def _(g):
            base = g * group
            at = pl.ds(pl.multiple_of(base * channels, span), span)
            right = pair_buf[:, :, part].reshape(-1, WIDTH)
            outer_scr[...] = jnp.dot(left(left_pair, at), right, preferred_element_type=jnp.float32)

            @pl.when(mask_on)
            def _():
                right = free_buf[:, :, part].reshape(-1, WIDTH)
                free_scr[...] = jnp.dot(left(left_free, at), right, preferred_element_type=jnp.float32)
                for i in range(group):
                    same = same_at(first, base + i)
                    piece = pl.ds(i * channels, channels)
                    for d in range(D_STEP):
                        at_lanes = pl.ds(d * LANES, LANES)
                        outer_scr[piece, at_lanes] += jnp.where(same, free_scr[piece, at_lanes], 0.0)

            project(w, outer_scr, total, base)

        pl.when(chunk == chunks - 1)(lambda: finish(tiles - 1))

    def help_compute(q):
        from_sibling(FREE, slot(q))
        w = weight[q]
        first = (1 - col) * tiles + tile_of(q * tiles, 1 - col)
        part = pl.ds(offset(slot(q)), WIDTH)

        @pl.when(q == 0)
        def _():
            help_acc[...] = jnp.zeros_like(help_acc)

        @pl.loop(0, rows // group)
        def _(g):
            base = g * group
            at = pl.ds(pl.multiple_of(base * channels, span), span)
            right = free_buf[:, :, part].reshape(-1, WIDTH)
            free_scr[...] = jnp.dot(left(left_free, at), right, preferred_element_type=jnp.float32)
            for i in range(group):
                same = same_at(first, base + i)
                piece = pl.ds(i * channels, channels)
                for d in range(D_STEP):
                    at_lanes = pl.ds(d * LANES, LANES)
                    free_scr[piece, at_lanes] = jnp.where(same, free_scr[piece, at_lanes], 0.0)
            project(w, free_scr, help_acc, base)

        @pl.when(q == steps - 1)
        def _():
            @pl.loop(0, rows)
            def _(i):
                count = paired_total + depth_ref[i].astype(jnp.float32)
                help_out[i] = (help_acc[i] * (1.0 / count)).T.astype(help_out.dtype)

            result_copy().start()

    def write(turn, helped):
        tile = tile_of(turn)

        @pl.loop(0, rows)
        def _(i):
            same = same_at(col * tiles + tile, i)
            count = paired_total + jnp.where(same, depth_ref[i].astype(jnp.float32), 0.0)
            value = (acc[turn, i] * (1.0 / count)).T
            if helped:
                value = value + help_out[i].astype(jnp.float32)
            if final:
                value = value + bias[...]
            out_ref[i, pl.ds(pl.multiple_of(tile * LANES, LANES), LANES), :] = value.astype(out_ref.dtype)

    def finish(turn):
        if share and turn == 0:
            @pl.when(asks)
            def _():
                result_copy().wait_recv()
                write(turn, True)

            pl.when(jnp.logical_not(asks))(functools.partial(write, turn, False))
        else:
            write(turn, False)

    def done_after(turn):
        return jnp.clip(turn - depth + 1, 0, chunks)

    @pl.loop(0, chunks + depth)
    def _(turn):
        relay(turn)

        @pl.when(turn == depth)
        def _():
            for c in left_copies:
                c.wait()
            for c in local:
                c.wait()
            guarded(unhelping, own_free.wait)

        if share:
            helping(turn - depth, lambda q: pl.when(helps)(lambda: help_compute(q)))

        @pl.loop(done_after(turn - 1), done_after(turn))
        def _(chunk):
            compute(chunk)

    @pl.loop(0, chunks)
    def _(chunk):
        drain(chunk)

    if share:
        pl.when(helps)(lambda: result_copy().wait_send())


def fused(right_pair, right_free, left_pair, left_free, weight, bias, start, end, depth, paired_total, final):
    count, width = lax.axis_size("row"), lax.axis_size("col")
    layers = count // (Y_SIZE * CORES)
    rows = start.shape[0]
    channels = left_pair.shape[0] // rows
    out_channels = weight.shape[1]
    cols = right_pair.shape[1] // channels
    tiles, steps = cols // LANES, channels // D_STEP
    chunks = tiles * steps
    group = min(16, rows)
    share = width == 2 and tiles == 2 and layers == width * tiles and rows * count == layers * LANES
    smem = pl.BlockSpec(memory_space=pltpu.SMEM)
    vmem = pl.BlockSpec(memory_space=pltpu.VMEM)
    anywhere = pl.BlockSpec(memory_space=pl.ANY)
    helped = (rows, out_channels, LANES) if share else (8, 8, LANES)
    return pl.pallas_call(
        functools.partial(fused_kernel, layers, width, group, float(paired_total), final, share),
        out_shape=jax.ShapeDtypeStruct((rows, cols, out_channels), jnp.bfloat16 if final else jnp.float32),
        in_specs=[smem] * 3 + [anywhere] * 4 + [vmem] * 2,
        out_specs=vmem,
        scratch_shapes=[
            pltpu.VMEM((count,) + right_pair.shape, jnp.bfloat16),
            pltpu.VMEM((count,) + right_free.shape, jnp.bfloat16),
            pltpu.VMEM((width,) + left_pair.shape, jnp.bfloat16),
            pltpu.VMEM((width,) + left_free.shape, jnp.bfloat16),
            pltpu.VMEM((group * channels, WIDTH), jnp.float32),
            pltpu.VMEM((group * channels, WIDTH), jnp.float32),
            pltpu.VMEM((tiles, rows, out_channels, LANES), jnp.float32),
            pltpu.VMEM(helped, jnp.float32),
            pltpu.VMEM((helped[0], helped[2], helped[1]), jnp.bfloat16),
            pltpu.VMEM((steps if share else 1, right_free.shape[0], WIDTH), jnp.bfloat16),
            pltpu.SemaphoreType.DMA((4, 2, chunks, count // CORES)),
            pltpu.SemaphoreType.DMA((2, chunks, count)),
            pltpu.SemaphoreType.DMA((2, width)),
            pltpu.SemaphoreType.DMA((2, width)),
            pltpu.SemaphoreType.DMA((4,)),
            pltpu.SemaphoreType.DMA((steps,)),
            pltpu.SemaphoreType.DMA((steps,)),
            pltpu.SemaphoreType.DMA((steps,)),
            pltpu.SemaphoreType.DMA((2,)),
        ],
        compiler_params=pltpu.CompilerParams(collective_id=0, has_side_effects=True, vmem_limit_bytes=60 << 20),
        name="gather_multiply",
    )(start, end, depth, right_pair, right_free, left_pair, left_free, weight, bias)


def flat_right(x):
    depth, channels, cols = x.shape
    return x.reshape(depth, channels, cols // LANES, LANES).transpose(0, 2, 1, 3).reshape(depth, -1)


def flat_left(x):
    depth, channels, rows = x.shape
    return x.transpose(2, 1, 0).reshape(rows * channels, depth)


def body(
    paired_left, paired_right, unpaired_left, unpaired_right,
    out_weight, out_bias, chain_lengths, unpaired_depths,
):
    channels, rows = paired_left.shape[1:]
    cols = paired_right.shape[2]
    first_row = lax.axis_index("row") * rows
    positions = first_row + jnp.arange(rows, dtype=jnp.int32)
    chains = jnp.arange(chain_lengths.shape[0])
    chain_ends = jnp.sum(
        jnp.where(chains[None, :] <= chains[:, None], chain_lengths[None, :], 0), axis=1, dtype=jnp.int32)
    chain_starts = chain_ends - chain_lengths
    inside = (positions[:, None] >= chain_starts[None, :]) & (positions[:, None] < chain_ends[None, :])

    def pick(table):
        return jnp.sum(jnp.where(inside, table[None, :], 0), axis=1, dtype=jnp.int32)

    depth = pick(unpaired_depths)
    start = pick(chain_starts)
    end = pick(chain_ends)

    seq = lax.axis_size("seq")
    free_here = unpaired_left.shape[0]
    first_free = (lax.axis_index("seq") * lax.axis_size("col") + lax.axis_index("col")) * free_here
    free_ids = first_free + jnp.arange(free_here, dtype=jnp.int32)
    live = free_ids[:, None] < depth[None, :]
    masked = jnp.where(live[:, None, :], unpaired_left, jnp.zeros((), unpaired_left.dtype))

    out_channels = out_weight.shape[1]
    weight = out_weight.reshape(channels, channels // D_STEP, D_STEP, out_channels).transpose(1, 3, 2, 0)
    weight = weight.reshape(channels // D_STEP, out_channels, D_STEP * channels)
    bias = out_bias.reshape(1, -1)
    paired_total = paired_right.shape[0] * lax.axis_size("row") * seq
    out = fused(
        flat_right(paired_right), flat_right(unpaired_right), flat_left(paired_left), flat_left(masked),
        weight, bias, start, end, depth, paired_total, seq == 1)
    if seq == 1:
        return out
    summed = lax.psum(out, "seq")
    share = cols // seq
    own = lax.dynamic_slice_in_dim(summed, lax.axis_index("seq") * share, share, 1)
    return (own + bias).astype(jnp.bfloat16)


def solution(mesh):
    return jax.shard_map(
        body,
        mesh=mesh,
        in_specs=(
            P(("groups", "seq", "col"), None, "row"),
            P(("groups", "seq", "row"), None, "col"),
            P(("groups", "seq", "col"), None, "row"),
            P(("groups", "seq", "row"), None, "col"),
            P(),
            P(),
            P("groups"),
            P("groups"),
        ),
        out_specs=P(("groups", "row"), ("col", "seq"), None),
        check_vma=False,
    )
```

time: 227 us -> 168 us (0.74)
  Pallas kernels: 211 us -> 153 us
    pallas_call x1, Pallas kernels: 211 us -> 153 us  [fused(): pl.pallas_call(functools.partial(fused_kernel, layers, width, group, floa...]
where the time goes in v1:
time: 168 us
  Pallas kernels  153 us (91%)
  local copies, waits for them, and re-layouts  11.9 us (7%)
  other arithmetic  3.05 us (2%)
    pallas_call x1, Pallas kernels, fused(): pl.pallas_call(functools.partial(fused_kernel, layers, width, group, floa...  153 us
    unnamed x11, local copies, waits for them, and re-layouts  5.98 us
    transpose x2, local copies, waits for them, and re-layouts, flat_left(): return x.transpose(2, 1, 0).reshape(rows * channels, depth)  3.71 us

profile of v1, /device:TPU:0, one launch (start us, length us, event | category | flops | bytes accessed | tf_op | source)
XLA Modules:
  0.0 167.8 jit_solution(3593492637035773326)
XLA Ops:
  0.0 0.0 copy-start
  0.0 0.0 copy-start.2
  0.0 0.9 select_reduce_fusion.3
  0.9 0.7 sub.3
  1.6 1.3 select_reduce_fusion
  2.9 0.0 copy-start.3
  2.9 0.1 broadcast_compare_fusion
  3.0 0.0 copy-start.1
  3.0 1.1 copy.29
  4.1 0.8 copy.30.weight
  5.0 2.1 %copy.27 = bf16[32,32,256]{2,1,0:T(8,128)(2,1)} copy(bf16[32,32,256]{2,0,1:T(8,128)(2,1)} %bitcast.39) | data formatting | bytes 1048576 | tf_op jit(solution)/shard_map/transpose | solution.py:514
  7.1 0.0 copy-done.2
  7.1 0.1 copy_bitcast_fusion.3
  7.2 1.1 copy.40
  8.4 0.0 copy-done.3
  8.4 0.0 copy-done.1
  8.4 0.1 select_bitcast_fusion
  8.4 1.6 copy.28
  10.0 0.0 copy-done
  10.0 0.2 copy_bitcast_fusion.1
  10.2 1.7 %copy.39 = bf16[8,8,64,128]{3,1,2,0:T(8,128)(2,1)} copy(bf16[8,8,64,128]{3,2,1,0:T(8,128)(2,1)S(1)} %bitcast.34) | data formatting | bytes 2097152
  11.9 152.8 %gather_multiply.1 = bf16[32,256,128]{2,1,0:T(8,128)(2,1)} custom-call(s32[32]{0:T(128)} %get-tuple-element.7.start_ref, s32[32]{0:T(128)} %get-tuple-element.6.end_ref, s32[32]{0:T(128)} %copy-done.3, bf16[32,8192]{1,0:T(8,128)(2,1)} %bitcast.36, bf16[64,8192]{1,0:T(8,128)(2,1)} %bitcast.33, bf16[1024,256]{1,0:T(8,128)(2,1)} %bitcast.35, ...), custom_call_target="tpu_custom_call" | custom-call | tf_op jit(solution)/shard_map/gather_multiply/pallas_call | solution.py:476
  164.7 3.1 %copy.42 = bf16[32,256,128]{2,1,0:T(8,128)(2,1)} copy(bf16[32,256,128]{2,1,0:T(8,128)(2,1)} %gather_multiply.1) | data formatting | bytes 4194304
  (2 shorter events, 0.0 us)
Async XLA Ops:
  0.0 10.0 %copy-start = (bf16[64,32,256]{2,1,0:T(8,128)(2,1)S(1)}, bf16[64,32,256]{2,1,0:T(8,128)(2,1)}, u32[]{:S(2)}) copy-start(bf16[64,32,256]{2,1,0:T(8,128)(2,1)} %param.11) | copy-start | bytes 3145732
  0.0 7.1 %copy-start.2 = (bf16[32,32,256]{2,1,0:T(8,128)(2,1)S(1)}, bf16[32,32,256]{2,1,0:T(8,128)(2,1)}, u32[]{:S(2)}) copy-start(bf16[32,32,256]{2,1,0:T(8,128)(2,1)} %param.9) | copy-start | bytes 1572868
  2.9 5.5 %copy-start.3 = (s32[32]{0:T(128)}, s32[32]{0:T(128)S(1)}, u32[]{:S(2)}) copy-start(s32[32]{0:T(128)S(1)} %get-tuple-element.5.depth_ref) | copy-start | bytes 388
  3.0 5.4 %copy-start.1 = (bf16[512,32,32]{0,2,1:T(8,128)(2,1)S(1)}, bf16[512,32,32]{0,2,1:T(8,128)(2,1)}, u32[]{:S(2)}) copy-start(bf16[512,32,32]{0,2,1:T(8,128)(2,1)} %param.10) | copy-start | bytes 3145732

commit v2 on v1

--- a/solution.py
+++ b/solution.py
@@ -14,6 +14,7 @@
 MESH = pl.DeviceIdType.MESH
 Y_SIZE, CORES = 2, 2
 AHEAD = 2
+HELP_LAG = 3
 PAIR_EARLY = 4
 UP, DOWN, ACROSS, SIBLING = range(4)
 PAIR, FREE = range(2)
@@ -35,9 +36,10 @@
 
 def fused_kernel(
     depth, width, group, paired_total, final, share,
-    start_ref, end_ref, depth_ref,
-    pair_in, free_in, left_pair_in, left_free_in, weight, bias,
+    lengths_ref, depths_ref,
+    pair_in, free_in, left_pair_in, left_free_in, plain_weight, bias,
     out_ref,
+    start_ref, end_ref, depth_ref, weight, wide_weight, spread, raw_pair, raw_free,
     pair_buf, free_buf, left_pair, left_free, outer_scr, free_scr, acc, help_acc, help_out, via_buf,
     send_sem, recv_sem, left_send, left_recv, local_sem, via_send, via_recv, pass_send, help_sem,
 ):
@@ -252,12 +254,14 @@
     def within(chunk, limit, do):
         pl.when((chunk >= 0) & (chunk < limit))(lambda: do(chunk))
 
-    def relay(turn):
+    def relay_line(turn):
         for hop in range(depth - 1, 0, -1):
             within(turn - (hop - 1), chunks, lambda chunk: arrivals(hop, y, chunk, onward(chunk, True)))
         if share:
             helping(turn, lambda part: help_first(part, True))
             helping(turn - 1, lambda part: help_line(part, True))
+
+    def relay_across(turn):
         for hop in range(depth - 1, -1, -1):
             within(turn - hop, chunks, lambda chunk: arrivals(hop, other, chunk, onward(chunk, True)))
         if share:
@@ -297,7 +301,7 @@
     local = [pltpu.make_async_copy(pair_in, pair_buf.at[row], local_sem.at[0])]
     own_free = pltpu.make_async_copy(free_in, free_buf.at[row], local_sem.at[1])
     unhelping = jnp.logical_not(helps) if share else True
-    for n, (source, out) in enumerate(((left_pair_in, left_pair), (left_free_in, left_free))):
+    for n, (source, out) in enumerate(((left_pair_in, raw_pair), (left_free_in, raw_free))):
         mine = out.at[col]
         for shift in range(1, width):
             c = pltpu.make_async_remote_copy(
@@ -310,6 +314,41 @@
         c.start()
     guarded(unhelping, own_free.start)
 
+    @pl.loop(0, rows)
+    def _(i):
+        place = row * rows + i
+        end, start, stop, deep = jnp.int32(0), jnp.int32(0), jnp.int32(0), jnp.int32(0)
+        for k in range(lengths_ref.shape[0]):
+            begin, end = end, end + lengths_ref[k]
+            mine = (place >= begin) & (place < end)
+            start = jnp.where(mine, begin, start)
+            stop = jnp.where(mine, end, stop)
+            deep = jnp.where(mine, depths_ref[k], deep)
+        start_ref[i], end_ref[i], depth_ref[i] = start, stop, deep
+
+    wide_weight[...] = plain_weight[...].astype(jnp.float32)
+    for step in range(steps):
+        picked = [wide_weight[pl.ds(step * D_STEP + d, channels, stride=channels), :] for d in range(D_STEP)]
+        weight[step] = jnp.concatenate(picked, axis=0).T.astype(jnp.bfloat16)
+
+    def arrange(raw, arranged, masked):
+        length = raw.shape[2]
+        wide = min(length, LANES)
+        for n in range(width):
+            for low in range(0, length, wide):
+                ids = lax.broadcasted_iota(jnp.int32, (1, LANES), 1) + n * length + low
+                if masked:
+                    ids = ids + lax.axis_index("seq") * (width * length)
+                spread[:, :wide] = raw[n, :, low:low + wide].astype(jnp.float32)
+
+                @pl.loop(0, rows, unroll=4)
+                def _(i):
+                    value = spread[pl.ds(i, channels, stride=rows), :]
+                    if masked:
+                        value = jnp.where(ids < depth_ref[i], value, 0.0)
+                    at = pl.ds(pl.multiple_of(i * channels, channels), channels)
+                    arranged[n, at, low:low + wide] = value[:, :wide].astype(jnp.bfloat16)
+
     def left(ref, at):
         return jnp.concatenate([ref[n, at, :] for n in range(width)], axis=1)
 
@@ -317,25 +356,40 @@
         lanes = lax.broadcasted_iota(jnp.int32, (1, LANES), 1) + first * LANES
         return (lanes >= start_ref[i]) & (lanes < end_ref[i])
 
-    def project(w, scratch, total, base):
+    def project(w, load, total, base):
         for pair in range(group // 2):
             halves = []
             for i in (2 * pair, 2 * pair + 1):
-                mine = scratch[pl.ds(i * channels, channels), :].astype(jnp.bfloat16)
-                halves.append(jnp.concatenate(
-                    [mine[:, d * LANES:(d + 1) * LANES] for d in range(D_STEP)], axis=0))
+                same = same_at(load.first, base + i) if load.masked else None
+                parts = []
+                for d in range(D_STEP):
+                    value = load(same, pl.ds(i * channels, channels), pl.ds(d * LANES, LANES))
+                    parts.append(value.astype(jnp.bfloat16))
+                halves.append(jnp.concatenate(parts, axis=0))
             projected = jnp.dot(w, jnp.concatenate(halves, axis=1), preferred_element_type=jnp.float32)
             for k in range(2):
                 total[base + 2 * pair + k] += projected[:, k * LANES:(k + 1) * LANES]
 
-    def compute(chunk):
-        if tiles > 1:
-            @pl.when(chunk == chunks - 1)
-            def _():
-                for done in range(tiles - 1):
-                    finish(done)
-
-        gathered(chunk)
+    class Load:
+        def __init__(self, first, paired, masked):
+            self.first, self.paired, self.masked = first, paired, masked
+
+        def __call__(self, same, piece, at):
+            value = 0.0
+            if self.masked:
+                value = jnp.where(same, free_scr[piece, at], 0.0)
+            if self.paired:
+                value = outer_scr[piece, at] + value
+            return value
+
+    def multiply(ref, buffer, part, base):
+        at = pl.ds(pl.multiple_of(base * channels, span), span)
+        right = buffer[:, :, part].reshape(-1, WIDTH)
+        return jnp.dot(left(ref, at), right, preferred_element_type=jnp.float32)
+
+    groups = rows // group
+
+    def compute(chunk, g):
         step = chunk // tiles
         turn = chunk % tiles
         first = col * tiles + tile_of(chunk)
@@ -343,112 +397,120 @@
         mask_on = needed(FREE, chunk)
         total = acc.at[turn]
         w = weight[step]
-
-        @pl.when(step == 0)
-        def _():
-            total[...] = jnp.zeros_like(total)
-
-        @pl.loop(0, rows // group)
-        def _(g):
-            base = g * group
-            at = pl.ds(pl.multiple_of(base * channels, span), span)
-            right = pair_buf[:, :, part].reshape(-1, WIDTH)
-            outer_scr[...] = jnp.dot(left(left_pair, at), right, preferred_element_type=jnp.float32)
-
-            @pl.when(mask_on)
+        base = g * group
+
+        @pl.when(g == 0)
+        def _():
+            gathered(chunk)
+
+            @pl.when(step == 0)
             def _():
-                right = free_buf[:, :, part].reshape(-1, WIDTH)
-                free_scr[...] = jnp.dot(left(left_free, at), right, preferred_element_type=jnp.float32)
-                for i in range(group):
-                    same = same_at(first, base + i)
-                    piece = pl.ds(i * channels, channels)
-                    for d in range(D_STEP):
-                        at_lanes = pl.ds(d * LANES, LANES)
-                        outer_scr[piece, at_lanes] += jnp.where(same, free_scr[piece, at_lanes], 0.0)
-
-            project(w, outer_scr, total, base)
-
-        pl.when(chunk == chunks - 1)(lambda: finish(tiles - 1))
-
-    def help_compute(q):
-        from_sibling(FREE, slot(q))
+                total[...] = jnp.zeros_like(total)
+
+        outer_scr[...] = multiply(left_pair, pair_buf, part, base)
+
+        @pl.when(mask_on)
+        def _():
+            free_scr[...] = multiply(left_free, free_buf, part, base)
+            project(w, Load(first, True, True), total, base)
+
+        @pl.when(jnp.logical_not(mask_on))
+        def _():
+            project(w, Load(first, True, False), total, base)
+
+    def help_compute(q, g):
         w = weight[q]
         first = (1 - col) * tiles + tile_of(q * tiles, 1 - col)
         part = pl.ds(offset(slot(q)), WIDTH)
-
-        @pl.when(q == 0)
-        def _():
-            help_acc[...] = jnp.zeros_like(help_acc)
-
-        @pl.loop(0, rows // group)
-        def _(g):
-            base = g * group
-            at = pl.ds(pl.multiple_of(base * channels, span), span)
-            right = free_buf[:, :, part].reshape(-1, WIDTH)
-            free_scr[...] = jnp.dot(left(left_free, at), right, preferred_element_type=jnp.float32)
-            for i in range(group):
-                same = same_at(first, base + i)
-                piece = pl.ds(i * channels, channels)
-                for d in range(D_STEP):
-                    at_lanes = pl.ds(d * LANES, LANES)
-                    free_scr[piece, at_lanes] = jnp.where(same, free_scr[piece, at_lanes], 0.0)
-            project(w, free_scr, help_acc, base)
-
-        @pl.when(q == steps - 1)
-        def _():
-            @pl.loop(0, rows)
+        base = g * group
+
+        @pl.when(g == 0)
+        def _():
+            from_sibling(FREE, slot(q))
+
+            @pl.when(q == 0)
+            def _():
+                help_acc[...] = jnp.zeros_like(help_acc)
+
+        free_scr[...] = multiply(left_free, free_buf, part, base)
+        project(w, Load(first, False, True), help_acc, base)
+
+        @pl.when((q == steps - 1) & (g == groups - 1))
+        def _():
+            @pl.loop(0, rows, unroll=4)
             def _(i):
                 count = paired_total + depth_ref[i].astype(jnp.float32)
                 help_out[i] = (help_acc[i] * (1.0 / count)).T.astype(help_out.dtype)
 
             result_copy().start()
 
-    def write(turn, helped):
-        tile = tile_of(turn)
+    def scaled(turn, i):
+        same = same_at(col * tiles + tile_of(turn), i)
+        count = paired_total + jnp.where(same, depth_ref[i].astype(jnp.float32), 0.0)
+        value = (acc[turn, i] * (1.0 / count)).T
+        return value + bias[...] if final else value
+
+    def store(turn, i, value):
+        at = pl.ds(pl.multiple_of(tile_of(turn) * LANES, LANES), LANES)
+        out_ref[i, at, :] = value.astype(out_ref.dtype)
+
+    def finish(turn):
+        def plain():
+            @pl.loop(0, rows, unroll=4)
+            def _(i):
+                store(turn, i, scaled(turn, i))
+
+        def hold():
+            @pl.loop(0, rows, unroll=4)
+            def _(i):
+                acc[turn, i] = scaled(turn, i)
+
+        if share and turn == 0:
+            pl.when(asks)(hold)
+            pl.when(jnp.logical_not(asks))(plain)
+        else:
+            plain()
+
+    def combine():
+        result_copy().wait_recv()
 
         @pl.loop(0, rows)
         def _(i):
-            same = same_at(col * tiles + tile, i)
-            count = paired_total + jnp.where(same, depth_ref[i].astype(jnp.float32), 0.0)
-            value = (acc[turn, i] * (1.0 / count)).T
-            if helped:
-                value = value + help_out[i].astype(jnp.float32)
-            if final:
-                value = value + bias[...]
-            out_ref[i, pl.ds(pl.multiple_of(tile * LANES, LANES), LANES), :] = value.astype(out_ref.dtype)
-
-    def finish(turn):
-        if share and turn == 0:
-            @pl.when(asks)
-            def _():
-                result_copy().wait_recv()
-                write(turn, True)
-
-            pl.when(jnp.logical_not(asks))(functools.partial(write, turn, False))
-        else:
-            write(turn, False)
-
-    def done_after(turn):
-        return jnp.clip(turn - depth + 1, 0, chunks)
+            store(0, i, acc[0, i] + help_out[i].astype(jnp.float32))
+
+    def work(turn, low, high):
+        @pl.loop(low, high)
+        def _(g):
+            if share:
+                helping(turn - HELP_LAG, lambda q: pl.when(helps)(lambda: help_compute(q, g)))
+            within(turn - depth, chunks, lambda chunk: compute(chunk, g))
+
+    start_at = min(depth, HELP_LAG)
 
     @pl.loop(0, chunks + depth)
     def _(turn):
-        relay(turn)
-
-        @pl.when(turn == depth)
+        relay_line(turn)
+        pl.when(turn > start_at)(lambda: work(turn, 0, groups // 2))
+        relay_across(turn)
+
+        @pl.when(turn == start_at)
         def _():
             for c in left_copies:
                 c.wait()
             for c in local:
                 c.wait()
             guarded(unhelping, own_free.wait)
-
-        if share:
-            helping(turn - depth, lambda q: pl.when(helps)(lambda: help_compute(q)))
-
-        @pl.loop(done_after(turn - 1), done_after(turn))
-        def _(chunk):
-            compute(chunk)
+            arrange(raw_pair, left_pair, False)
+            arrange(raw_free, left_free, True)
+            work(turn, 0, groups // 2)
+
+        work(turn, groups // 2, groups)
+
+        for done in range(tiles):
+            pl.when(turn == chunks + depth - tiles + done)(functools.partial(finish, done))
+
+    if share:
+        pl.when(asks)(combine)
 
     @pl.loop(0, chunks)
     def _(chunk):
@@ -458,10 +520,9 @@
         pl.when(helps)(lambda: result_copy().wait_send())
 
 
-def fused(right_pair, right_free, left_pair, left_free, weight, bias, start, end, depth, paired_total, final):
+def fused(right_pair, right_free, left_pair, left_free, weight, bias, lengths, depths, rows, paired_total, final):
     count, width = lax.axis_size("row"), lax.axis_size("col")
     layers = count // (Y_SIZE * CORES)
-    rows = start.shape[0]
     channels = left_pair.shape[0] // rows
     out_channels = weight.shape[1]
     cols = right_pair.shape[1] // channels
@@ -476,9 +537,17 @@
     return pl.pallas_call(
         functools.partial(fused_kernel, layers, width, group, float(paired_total), final, share),
         out_shape=jax.ShapeDtypeStruct((rows, cols, out_channels), jnp.bfloat16 if final else jnp.float32),
-        in_specs=[smem] * 3 + [anywhere] * 4 + [vmem] * 2,
+        in_specs=[smem] * 2 + [anywhere] * 4 + [vmem] * 2,
         out_specs=vmem,
         scratch_shapes=[
+            pltpu.SMEM((rows,), jnp.int32),
+            pltpu.SMEM((rows,), jnp.int32),
+            pltpu.SMEM((rows,), jnp.int32),
+            pltpu.VMEM((steps, out_channels, D_STEP * channels), jnp.bfloat16),
+            pltpu.VMEM(weight.shape, jnp.float32),
+            pltpu.VMEM((left_pair.shape[0], LANES), jnp.float32),
+            pltpu.VMEM((width,) + left_pair.shape, jnp.bfloat16),
+            pltpu.VMEM((width,) + left_free.shape, jnp.bfloat16),
             pltpu.VMEM((count,) + right_pair.shape, jnp.bfloat16),
             pltpu.VMEM((count,) + right_free.shape, jnp.bfloat16),
             pltpu.VMEM((width,) + left_pair.shape, jnp.bfloat16),
@@ -501,7 +570,7 @@
         ],
         compiler_params=pltpu.CompilerParams(collective_id=0, has_side_effects=True, vmem_limit_bytes=60 << 20),
         name="gather_multiply",
-    )(start, end, depth, right_pair, right_free, left_pair, left_free, weight, bias)
+    )(lengths, depths, right_pair, right_free, left_pair, left_free, weight, bias)
 
 
 def flat_right(x):
@@ -511,45 +580,21 @@
 
 def flat_left(x):
     depth, channels, rows = x.shape
-    return x.transpose(2, 1, 0).reshape(rows * channels, depth)
+    return x.transpose(1, 2, 0).reshape(channels * rows, depth)
 
 
 def body(
     paired_left, paired_right, unpaired_left, unpaired_right,
     out_weight, out_bias, chain_lengths, unpaired_depths,
 ):
-    channels, rows = paired_left.shape[1:]
+    rows = paired_left.shape[2]
     cols = paired_right.shape[2]
-    first_row = lax.axis_index("row") * rows
-    positions = first_row + jnp.arange(rows, dtype=jnp.int32)
-    chains = jnp.arange(chain_lengths.shape[0])
-    chain_ends = jnp.sum(
-        jnp.where(chains[None, :] <= chains[:, None], chain_lengths[None, :], 0), axis=1, dtype=jnp.int32)
-    chain_starts = chain_ends - chain_lengths
-    inside = (positions[:, None] >= chain_starts[None, :]) & (positions[:, None] < chain_ends[None, :])
-
-    def pick(table):
-        return jnp.sum(jnp.where(inside, table[None, :], 0), axis=1, dtype=jnp.int32)
-
-    depth = pick(unpaired_depths)
-    start = pick(chain_starts)
-    end = pick(chain_ends)
-
     seq = lax.axis_size("seq")
-    free_here = unpaired_left.shape[0]
-    first_free = (lax.axis_index("seq") * lax.axis_size("col") + lax.axis_index("col")) * free_here
-    free_ids = first_free + jnp.arange(free_here, dtype=jnp.int32)
-    live = free_ids[:, None] < depth[None, :]
-    masked = jnp.where(live[:, None, :], unpaired_left, jnp.zeros((), unpaired_left.dtype))
-
-    out_channels = out_weight.shape[1]
-    weight = out_weight.reshape(channels, channels // D_STEP, D_STEP, out_channels).transpose(1, 3, 2, 0)
-    weight = weight.reshape(channels // D_STEP, out_channels, D_STEP * channels)
     bias = out_bias.reshape(1, -1)
     paired_total = paired_right.shape[0] * lax.axis_size("row") * seq
     out = fused(
-        flat_right(paired_right), flat_right(unpaired_right), flat_left(paired_left), flat_left(masked),
-        weight, bias, start, end, depth, paired_total, seq == 1)
+        flat_right(paired_right), flat_right(unpaired_right), flat_left(paired_left), flat_left(unpaired_left),
+        out_weight, bias, chain_lengths, unpaired_depths, rows, paired_total, seq == 1)
     if seq == 1:
         return out
     summed = lax.psum(out, "seq")

time: 168 us -> 142 us (0.85)
  Pallas kernels: 153 us -> 134 us
  local copies, waits for them, and re-layouts: 11.9 us -> 7.39 us
  other arithmetic: 3.05 us -> 0 us
    pallas_call x1, Pallas kernels: 153 us -> 134 us  [fused(): pl.pallas_call(functools.partial(fused_kernel, layers, width, group, floa...]
    transpose x3 -> x0, local copies, waits for them, and re-layouts: 4.85 us -> none  [the longest x2 3.71 us: flat_left(): return x.transpose(2, 1, 0).reshape(rows * channels, depth)]
    reduce_sum x2 -> x0, other arithmetic: 2.23 us -> none  [the longest x1 1.34 us: pick(): jnp.sum(jnp.where(inside, table[None, :], 0), axis=1, dtype=jnp.int32)]
    unnamed x11 -> x5, local copies, waits for them, and re-layouts: 5.98 us -> 5.97 us
where the time goes in v2:
time: 142 us; the launch traced here: 141 us
  Pallas kernels  134 us (94%)
  local copies, waits for them, and re-layouts  7.39 us (5%)
    pallas_call x1, Pallas kernels, fused(): pl.pallas_call(functools.partial(fused_kernel, layers, width, group, floa...  134 us
    unnamed x5, local copies, waits for them, and re-layouts  5.97 us

profile of v2, /device:TPU:0, one launch (start us, length us, event | category | flops | bytes accessed | tf_op | source)
XLA Modules:
  0.0 141.4 jit_solution(7708725101634104939)
XLA Ops:
  0.0 0.0 copy-start
  0.0 1.2 copy_bitcast_fusion.3
  1.2 1.1 copy.20
  2.4 0.0 copy-done
  2.4 0.2 copy_bitcast_fusion.1
  2.6 1.7 %copy.19 = bf16[8,8,64,128]{3,1,2,0:T(8,128)(2,1)} copy(bf16[8,8,64,128]{3,2,1,0:T(8,128)(2,1)S(1)} %bitcast.30) | data formatting | bytes 2097152
  4.3 134.0 %gather_multiply.1 = bf16[32,256,128]{2,1,0:T(8,128)(2,1)} custom-call(s32[12]{0:T(128)} %lengths_ref.1, s32[12]{0:T(128)} %depths_ref.1, bf16[32,8192]{1,0:T(8,128)(2,1)} %bitcast.31, bf16[64,8192]{1,0:T(8,128)(2,1)} %bitcast.29, bf16[1024,256]{1,0:T(8,128)(2,1)} %bitcast.34, bf16[1024,512]{1,0:T(8,128)(2,1)} %bitcast.33, bf16[1024,128]{1,0:T(8,128)(2,1)} %plain_weight.1, ...), custom_call_target="tpu_custom_call" | custom-call | tf_op jit(solution)/shard_map/gather_multiply/pallas_call | solution.py:537
  138.2 3.1 %copy.22 = bf16[32,256,128]{2,1,0:T(8,128)(2,1)} copy(bf16[32,256,128]{2,1,0:T(8,128)(2,1)} %gather_multiply.1) | data formatting | bytes 4194304
Async XLA Ops:
  0.0 2.4 %copy-start = (bf16[64,32,256]{2,1,0:T(8,128)(2,1)S(1)}, bf16[64,32,256]{2,1,0:T(8,128)(2,1)}, u32[]{:S(2)}) copy-start(bf16[64,32,256]{2,1,0:T(8,128)(2,1)} %param.11) | copy-start | bytes 3145732

commit v3 on v2

--- a/solution.py
+++ b/solution.py
@@ -255,14 +255,14 @@
         pl.when((chunk >= 0) & (chunk < limit))(lambda: do(chunk))
 
     def relay_line(turn):
-        for hop in range(depth - 1, 0, -1):
+        for hop in range(1, depth):
             within(turn - (hop - 1), chunks, lambda chunk: arrivals(hop, y, chunk, onward(chunk, True)))
         if share:
             helping(turn, lambda part: help_first(part, True))
             helping(turn - 1, lambda part: help_line(part, True))
 
     def relay_across(turn):
-        for hop in range(depth - 1, -1, -1):
+        for hop in range(depth):
             within(turn - hop, chunks, lambda chunk: arrivals(hop, other, chunk, onward(chunk, True)))
         if share:
             helping(turn - 2, lambda part: help_last(part, True))
@@ -341,7 +341,7 @@
                     ids = ids + lax.axis_index("seq") * (width * length)
                 spread[:, :wide] = raw[n, :, low:low + wide].astype(jnp.float32)
 
-                @pl.loop(0, rows, unroll=4)
+                @pl.loop(0, rows, unroll=8)
                 def _(i):
                     value = spread[pl.ds(i, channels, stride=rows), :]
                     if masked:
@@ -437,7 +437,7 @@
 
         @pl.when((q == steps - 1) & (g == groups - 1))
         def _():
-            @pl.loop(0, rows, unroll=4)
+            @pl.loop(0, rows, unroll=8)
             def _(i):
                 count = paired_total + depth_ref[i].astype(jnp.float32)
                 help_out[i] = (help_acc[i] * (1.0 / count)).T.astype(help_out.dtype)
@@ -456,12 +456,12 @@
 
     def finish(turn):
         def plain():
-            @pl.loop(0, rows, unroll=4)
+            @pl.loop(0, rows, unroll=8)
             def _(i):
                 store(turn, i, scaled(turn, i))
 
         def hold():
-            @pl.loop(0, rows, unroll=4)
+            @pl.loop(0, rows, unroll=8)
             def _(i):
                 acc[turn, i] = scaled(turn, i)
 

time: 142 us -> 141 us (level)
  no operation moved by 1% of the time
where the time goes in v3:
time: 141 us
  Pallas kernels  134 us (95%)
  local copies, waits for them, and re-layouts  7.39 us (5%)
    pallas_call x1, Pallas kernels, fused(): pl.pallas_call(functools.partial(fused_kernel, layers, width, group, floa...  134 us
    unnamed x5, local copies, waits for them, and re-layouts  5.97 us

profile of v3, /device:TPU:0, one launch (start us, length us, event | category | flops | bytes accessed | tf_op | source)
XLA Modules:
  0.0 140.9 jit_solution(17726642556884722255)
XLA Ops:
  0.0 0.0 copy-start
  0.0 1.2 copy_bitcast_fusion.3
  1.2 1.1 copy.20
  2.4 0.0 copy-done
  2.4 0.2 copy_bitcast_fusion.1
  2.6 1.7 %copy.19 = bf16[8,8,64,128]{3,1,2,0:T(8,128)(2,1)} copy(bf16[8,8,64,128]{3,2,1,0:T(8,128)(2,1)S(1)} %bitcast.30) | data formatting | bytes 2097152
  4.3 133.5 %gather_multiply.1 = bf16[32,256,128]{2,1,0:T(8,128)(2,1)} custom-call(s32[12]{0:T(128)} %lengths_ref.1, s32[12]{0:T(128)} %depths_ref.1, bf16[32,8192]{1,0:T(8,128)(2,1)} %bitcast.31, bf16[64,8192]{1,0:T(8,128)(2,1)} %bitcast.29, bf16[1024,256]{1,0:T(8,128)(2,1)} %bitcast.34, bf16[1024,512]{1,0:T(8,128)(2,1)} %bitcast.33, bf16[1024,128]{1,0:T(8,128)(2,1)} %plain_weight.1, ...), custom_call_target="tpu_custom_call" | custom-call | tf_op jit(solution)/shard_map/gather_multiply/pallas_call | solution.py:537
  137.8 3.1 %copy.22 = bf16[32,256,128]{2,1,0:T(8,128)(2,1)} copy(bf16[32,256,128]{2,1,0:T(8,128)(2,1)} %gather_multiply.1) | data formatting | bytes 4194304
Async XLA Ops:
  0.0 2.4 %copy-start = (bf16[64,32,256]{2,1,0:T(8,128)(2,1)S(1)}, bf16[64,32,256]{2,1,0:T(8,128)(2,1)}, u32[]{:S(2)}) copy-start(bf16[64,32,256]{2,1,0:T(8,128)(2,1)} %param.11) | copy-start | bytes 3145732
